TPU v7x, 8 devices: a whole 2x2x1 slice. The times are simulated.
8 devices in a mesh: proto: 4 (over z, y, x), data: 2 (over core).
Axes of the slice: x: 2, y: 2, z: 1, core: 2. Of those that a mesh axis runs over, the one named last changes fastest.
Arguments:
- emb_one: bfloat16 [4096, 256], P('data')
- emb_two: bfloat16 [4096, 256], P('data')
- protos: bfloat16 [1024, 256], P('proto')
Outputs:
- output 1: float32 [4096, 1024], P('data', 'proto')
- output 2: float32 [4096, 1024], P('data', 'proto')
- output 3: float32 [], replicated
- output 4: float32 [4096, 256], P('data')
- output 5: float32 [4096, 256], P('data')
- output 6: float32 [1024, 256], P('proto')
All inputs are finite; a program needn't handle non-finite values.
Results may differ from a plain program's by a relative error of at most 0.001.
Values are sent between devices in bfloat16 or wider.
A program may use at most 1 GiB of HBM per device.

v0:
```python
import jax
import jax.numpy as jnp
from jax import lax
from jax.sharding import PartitionSpec as P, NamedSharding

EPSILON = 0.05
TEMP_TAU = 0.1
value_a14 = 3


def solution(mesh):
    proto_size = mesh.shape['proto']
    data_size = mesh.shape['data']

    def local_step(emb_one, emb_two, protos):
        local_rows = emb_one.shape[0]
        total_rows = local_rows * data_size
        total_protos = protos.shape[0] * proto_size

        def view_terms(emb):
            scores = jnp.einsum('nd,kd->nk', emb, protos, preferred_element_type=jnp.float32)
            transport = jnp.exp(scores / EPSILON)
            for _ in range(value_a14):
                col_sum = lax.psum(jnp.sum(transport, axis=0), 'data')
                transport = transport / (total_protos * col_sum)
                row_sum = lax.psum(jnp.sum(transport, axis=1, keepdims=True), 'proto')
                transport = transport / (total_rows * row_sum)
            codes = total_rows * transport
            logits = scores / TEMP_TAU
            soft_denom = lax.psum(jnp.sum(jnp.exp(logits), axis=1, keepdims=True), 'proto')
            return codes, logits - jnp.log(soft_denom)

        codes_one, logp_one = view_terms(emb_one)
        codes_two, logp_two = view_terms(emb_two)
        part_loss = jnp.sum(codes_two * logp_one) + jnp.sum(codes_one * logp_two)
        loss_value = -lax.psum(part_loss, ('proto', 'data')) / (2 * total_rows)
        grad_scale = 2 * total_rows * TEMP_TAU
        logit_grad_one = ((jnp.exp(logp_one) - codes_two) / grad_scale).astype(jnp.bfloat16)
        logit_grad_two = ((jnp.exp(logp_two) - codes_one) / grad_scale).astype(jnp.bfloat16)
        grad_one = lax.psum(jnp.einsum('nk,kd->nd', logit_grad_one, protos, preferred_element_type=jnp.float32), 'proto')
        grad_two = lax.psum(jnp.einsum('nk,kd->nd', logit_grad_two, protos, preferred_element_type=jnp.float32), 'proto')
        proto_part = (jnp.einsum('nk,nd->kd', logit_grad_one, emb_one, preferred_element_type=jnp.float32)
                      + jnp.einsum('nk,nd->kd', logit_grad_two, emb_two, preferred_element_type=jnp.float32))
        grad_protos = lax.psum(proto_part, 'data')
        return codes_one, codes_two, loss_value, grad_one, grad_two, grad_protos

    return jax.shard_map(
        local_step, mesh=mesh,
        in_specs=(P('data', None), P('data', None), P('proto', None)),
        out_specs=(P('data', 'proto'), P('data', 'proto'), P(), P('data', None), P('data', None), P('proto', None)),
        check_vma=False)
```

profile of v0, /device:TPU:0, one launch (start us, length us, event | category | flops | bytes accessed | tf_op | source)
XLA Modules:
  0.0 239.9 jit_solution(9725011329736583776)
XLA Ops:
  7.2 0.0 copy-start
  7.2 0.0 all-reduce.7.cloned.1.call-start
  7.2 1.9 fusion.24
  9.1 3.0 %psum.126 = f32[256]{0:T(256)S(1)} all-reduce(f32[256]{0:T(256)S(1)} %get-tuple-element.36), channel_id=1, replica_groups=mesh['proto'=4,'data'=2] {'data'}, use_global_device_ids=true, to_apply=%region_1.0 | all-reduce | flops 256 | bytes 2048 | tf_op jit(solution)/shard_map/psum | solution.py:24
  12.1 0.7 exponential_reduce_fusion.1
  12.8 11.4 %psum.127 = f32[2048,1]{0,1:T(1,128)S(1)} all-reduce(f32[2048,1]{0,1:T(1,128)S(1)} %bitcast.52), channel_id=1, replica_groups=mesh['proto'=4,'data'=2] {'proto'}, use_global_device_ids=true, to_apply=%region_3.0 | all-reduce | flops 2048 | bytes 16384 | tf_op jit(solution)/shard_map/psum | solution.py:26
  24.2 0.6 fusion.16
  24.8 2.5 %psum.128 = f32[256]{0:T(256)S(1)} all-reduce(f32[256]{0:T(256)S(1)} %fusion.16), channel_id=1, replica_groups=mesh['proto'=4,'data'=2] {'data'}, use_global_device_ids=true, to_apply=%region_5.0 | all-reduce | flops 256 | bytes 2048 | tf_op jit(solution)/shard_map/psum | solution.py:24
  27.3 0.6 fusion.19
  27.9 8.1 %psum.129 = f32[2048,1]{0,1:T(1,128)S(1)} all-reduce(f32[2048,1]{0,1:T(1,128)S(1)} %bitcast.53), channel_id=1, replica_groups=mesh['proto'=4,'data'=2] {'proto'}, use_global_device_ids=true, to_apply=%region_7.0 | all-reduce | flops 2048 | bytes 16384 | tf_op jit(solution)/shard_map/psum | solution.py:26
  36.0 0.7 fusion.20
  36.7 2.1 exponential_reduce_fusion
  38.8 2.4 %all-reduce.3 = (f32[256]{0:T(256)S(1)}, f32[256]{0:T(256)S(1)}) all-reduce(f32[256]{0:T(256)S(1)} %fusion.20, f32[256]{0:T(256)S(1)} %get-tuple-element.21), channel_id=1, replica_groups=mesh['proto'=4,'data'=2] {'data'}, use_global_device_ids=true, to_apply=%region_9.0 | all-reduce | flops 512 | bytes 4096 | tf_op jit(solution)/shard_map/psum | solution.py:24
  41.2 0.8 fusion.23
  42.1 15.2 %all-reduce.1 = (f32[2048,1]{0,1:T(1,128)S(1)}, f32[2048,1]{0,1:T(1,128)S(1)}) all-reduce(f32[2048,1]{0,1:T(1,128)S(1)} %bitcast.50, f32[2048,1]{0,1:T(1,128)S(1)} %bitcast.57), channel_id=1, replica_groups=mesh['proto'=4,'data'=2] {'proto'}, use_global_device_ids=true, to_apply=%region_11.0 | all-reduce | flops 4096 | bytes 32768 | tf_op jit(solution)/shard_map/psum | solution.py:26
  57.3 0.0 copy-start.1
  57.3 4.3 %multiply_convert_fusion = (bf16[2048,256]{0,1:T(8,128)(2,1)}, f32[2048,256]{0,1:T(8,128)S(1)}) fusion(f32[2048,256]{0,1:T(8,128)} %get-tuple-element.38, f32[2048]{0:T(1024)S(1)} %bitcast.46, f32[2048]{0:T(1024)S(1)} %bitcast.55, f32[256]{0:T(256)S(1)} %get-tuple-element.40, f32[2048]{0:T(1024)S(1)} %bitcast.40, f32[256]{0:T(256)S(1)} %broadcast_multiply_fusion.10, ...), kind=kLoop, calls=%fused_computation.20 | loop fusion | flops 6815744 | bytes 7375872 | tf_op jit(solution)/shard_map/convert_element_type | solution.py:39
  61.6 1.4 multiply_reduce_fusion
  63.0 8.0 %psum.133 = f32[2048,1]{0,1:T(1,128)S(1)} all-reduce(f32[2048,1]{0,1:T(1,128)S(1)} %bitcast.51), channel_id=1, replica_groups=mesh['proto'=4,'data'=2] {'proto'}, use_global_device_ids=true, to_apply=%region_15.0 | all-reduce | flops 2048 | bytes 16384 | tf_op jit(solution)/shard_map/psum | solution.py:26
  71.0 2.2 fusion.17
  73.2 2.5 %psum.134 = f32[256]{0:T(256)S(1)} all-reduce(f32[256]{0:T(256)S(1)} %fusion.17), channel_id=1, replica_groups=mesh['proto'=4,'data'=2] {'data'}, use_global_device_ids=true, to_apply=%region_17.0 | all-reduce | flops 256 | bytes 2048 | tf_op jit(solution)/shard_map/psum | solution.py:24
  75.7 2.2 fusion.18
  77.8 10.0 %psum.135 = f32[2048,1]{0,1:T(1,128)S(1)} all-reduce(f32[2048,1]{0,1:T(1,128)S(1)} %bitcast.54), channel_id=1, replica_groups=mesh['proto'=4,'data'=2] {'proto'}, use_global_device_ids=true, to_apply=%region_19.0 | all-reduce | flops 2048 | bytes 16384 | tf_op jit(solution)/shard_map/psum | solution.py:26
  87.9 2.3 fusion.21
  90.2 2.5 %psum.136 = f32[256]{0:T(256)S(1)} all-reduce(f32[256]{0:T(256)S(1)} %fusion.21), channel_id=1, replica_groups=mesh['proto'=4,'data'=2] {'data'}, use_global_device_ids=true, to_apply=%region_21.0 | all-reduce | flops 256 | bytes 2048 | tf_op jit(solution)/shard_map/psum | solution.py:24
  92.7 2.4 %fusion.22 = f32[2048]{0:T(1024)S(1)} fusion(f32[256]{0:T(256)S(1)} %broadcast_multiply_fusion.6, f32[2048]{0:T(1024)S(1)} %bitcast.42, f32[256]{0:T(256)S(1)} %broadcast_multiply_fusion.7, f32[2048]{0:T(1024)S(1)} %bitcast.36, f32[256]{0:T(256)S(1)} %get-tuple-element.39, f32[2048,256]{0,1:T(8,128)} %get-tuple-element.38), kind=kLoop, calls=%fused_computation.36 | loop fusion | flops 3667968 | bytes 2124800 | tf_op jit(solution)/shard_map/reduce_sum | solution.py:26
  95.1 13.9 %all-reduce = (f32[2048,1]{0,1:T(1,128)S(1)}, f32[2048,1]{0,1:T(1,128)S(1)}) all-reduce(f32[2048,1]{0,1:T(1,128)S(1)} %bitcast.49, f32[2048,1]{0,1:T(1,128)S(1)} %bitcast.48), channel_id=1, replica_groups=mesh['proto'=4,'data'=2] {'proto'}, use_global_device_ids=true, to_apply=%region_23.0 | all-reduce | flops 4096 | bytes 32768 | tf_op jit(solution)/shard_map/psum | solution.py:26
  109.1 0.0 copy-start.7
  109.1 4.6 %multiply_convert_fusion.1 = (bf16[2048,256]{0,1:T(8,128)(2,1)S(1)}, f32[2048,256]{0,1:T(8,128)}) fusion(f32[2048,256]{0,1:T(8,128)S(1)} %get-tuple-element.37, f32[2048]{0:T(1024)S(1)} %bitcast.44, f32[2048]{0:T(1024)S(1)} %bitcast.56, f32[256]{0:T(256)S(1)} %broadcast_multiply_fusion.6, f32[2048]{0:T(1024)S(1)} %bitcast.43, ...), kind=kLoop, calls=%fused_computation.21 | loop fusion | flops 6815744 | bytes 7375872 | tf_op jit(solution)/shard_map/convert_element_type | solution.py:38
  113.6 1.0 copy-done.5
  114.6 0.4 fusion.30
  115.0 0.2 copy-done.4
  115.2 1.1 convolution_add_fusion
  116.4 0.0 all-reduce.7.cloned.1.call-update
  116.4 0.0 all-reduce.9.cloned.1.call-start
  116.5 0.0 copy-start.6
  116.5 3.1 %fusion.29 = f32[2048,256]{1,0:T(8,128)} fusion(bf16[2048,256]{0,1:T(8,128)(2,1)} %get-tuple-element.32, bf16[256,256]{1,0:T(8,128)(2,1)S(1)} %copy-done.9), kind=kOutput, calls=%fused_computation.54 | convolution fusion | flops 268435456 | bytes 3276800 | tf_op jit(solution)/shard_map/nk,kd->nd/dot_general | solution.py:41
  119.6 1.8 fusion.28
  121.4 0.0 all-reduce.9.cloned.1.call-update
  121.5 2.7 %multiply_reduce_fusion.1 = f32[]{:T(128)} fusion(f32[2048,256]{0,1:T(8,128)} %get-tuple-element.35, f32[2048,256]{0,1:T(8,128)S(1)} %get-tuple-element.37, f32[2048]{0:T(1024)S(1)} %bitcast.45), kind=kLoop, calls=%fused_computation.24 | loop fusion | flops 2097151 | bytes 4202500 | tf_op jit(solution)/shard_map/reduce_sum | solution.py:35
  125.5 22.9 %psum.140 = f32[]{:T(128)} all-reduce(f32[]{:T(128)S(6)} %add.42), channel_id=1, replica_groups=mesh['proto'=4,'data'=2] {'proto','data'}, use_global_device_ids=true, to_apply=%region_30.0 | all-reduce | flops 1 | bytes 8 | tf_op jit(solution)/shard_map/psum | solution.py:36
  148.4 3.0 %copy.11 = f32[2048,256]{1,0:T(8,128)} copy(f32[2048,256]{0,1:T(8,128)} %copy-done.2) | data formatting | bytes 4194304
  151.4 1.8 copy.12
  153.9 0.0 all-reduce.7.cloned.1.call-done
  153.9 72.8 %all-reduce.9.cloned.1.call-done = (f32[2048,256]{1,0:T(8,128)}, f32[2048,256]{1,0:T(8,128)}) async-done(((f32[2048,256]{1,0:T(8,128)}, f32[2048,256]{1,0:T(8,128)}), (f32[2048,256]{1,0:T(8,128)}, f32[2048,256]{1,0:T(8,128)})) %all-reduce.9.cloned.1.call-update) | async-done | bytes 4194320 | tf_op jit(solution)/shard_map/psum | solution.py:40
  226.7 3.2 %copy.16 = f32[2048,256]{1,0:T(8,128)} copy(f32[2048,256]{1,0:T(8,128)} %get-tuple-element.44) | data formatting | bytes 4194304
  229.9 1.3 copy.17
  231.2 0.7 copy.18
  (29 shorter events, 0.2 us)
Async XLA Ops:
  7.2 29.6 %copy-start = (bf16[2048,256]{1,0:T(8,128)(2,1)S(1)}, bf16[2048,256]{1,0:T(8,128)(2,1)}, u32[]{:S(2)}) copy-start(bf16[2048,256]{1,0:T(8,128)(2,1)} %param.4) | copy-start | bytes 3145732
  7.2 146.7 %all-reduce.7.cloned.1.call-start = ((), (), s32[]{:S(2)}) async-start(), calls=%async_computation | async-start | bytes 524288 | tf_op jit(solution)/shard_map/psum | solution.py:44
  27.3 9.4 %copy-start.9 = (bf16[256,256]{1,0:T(8,128)(2,1)S(1)}, bf16[256,256]{1,0:T(8,128)(2,1)}, u32[]{:S(2)}) copy-start(bf16[256,256]{1,0:T(8,128)(2,1)} %param.5) | copy-start | bytes 393220
  57.3 4.3 %copy-start.1 = (f32[2048,256]{0,1:T(8,128)S(1)}, f32[2048,256]{0,1:T(8,128)}, u32[]{:S(2)}) copy-start(f32[2048,256]{0,1:T(8,128)} %get-tuple-element.38) | copy-start | bytes 6291460
  61.6 1.4 copy-start.2
  109.1 5.5 %copy-start.7 = (bf16[2048,256]{1,0:T(8,128)(2,1)S(1)}, bf16[2048,256]{1,0:T(8,128)(2,1)}, u32[]{:S(2)}) copy-start(bf16[2048,256]{1,0:T(8,128)(2,1)} %param.3) | copy-start | bytes 3145732
  113.6 1.0 copy-start.5
  113.6 1.6 copy-start.4
  116.4 110.3 %all-reduce.9.cloned.1.call-start = ((), (), s32[]{:S(2)}) async-start(), calls=%async_computation.1 | async-start | bytes 8388608 | tf_op jit(solution)/shard_map/psum | solution.py:40
  116.5 3.2 %copy-start.6 = (bf16[2048,256]{0,1:T(8,128)(2,1)S(1)}, bf16[2048,256]{0,1:T(8,128)(2,1)}, u32[]{:S(2)}) copy-start(bf16[2048,256]{0,1:T(8,128)(2,1)} %copy-done.5) | copy-start | bytes 3145732
  148.4 3.0 %copy-start.3 = (f32[2048,256]{0,1:T(8,128)S(1)}, f32[2048,256]{0,1:T(8,128)}, u32[]{:S(2)}) copy-start(f32[2048,256]{0,1:T(8,128)} %get-tuple-element.35) | copy-start | bytes 6291460
  226.7 3.2 %copy-start.8 = (f32[2048,256]{1,0:T(8,128)S(1)}, f32[2048,256]{1,0:T(8,128)}, u32[]{:S(2)}) copy-start(f32[2048,256]{1,0:T(8,128)} %get-tuple-element.45) | copy-start | bytes 6291460
  229.9 1.3 copy-start.10
Sparse Core Ops, SparseCore 0:
  116.5 12.6 all-reduce.6
  132.7 93.9 all-reduce.8
where the time goes:
time: 240 us
  blocking collectives  102 us (42%)
  waiting for transfers between devices  72.8 us (30%)
  other arithmetic  25.6 us (11%)
  between operations  17.3 us (7%)
  local copies, waits for them, and re-layouts  11.3 us (5%)
  matrix products  10.5 us (4%)
    psum x1, waiting for transfers between devices, local_step(): lax.psum(jnp.einsum('nk,kd->nd', logit_grad_one, protos, preferred_elemen...  72.8 us
    psum x6, blocking collectives, view_terms(): row_sum = lax.psum(jnp.sum(transport, axis=1, keepdims=True), 'proto')  66.5 us
    psum x1, blocking collectives, local_step(): loss_value = -lax.psum(part_loss, ('proto', 'data')) / (2 * total_rows)  22.9 us
    psum x5, blocking collectives, view_terms(): col_sum = lax.psum(jnp.sum(transport, axis=0), 'data')  12.8 us
    unnamed x27, local copies, waits for them, and re-layouts  11.3 us
    reduce_sum x4, other arithmetic, view_terms(): row_sum = lax.psum(jnp.sum(transport, axis=1, keepdims=True), 'proto')  6 us
    reduce_sum x4, other arithmetic, view_terms(): col_sum = lax.psum(jnp.sum(transport, axis=0), 'data')  5.92 us
  transfers between devices with their start and end apart: 2, of which 1 were waited for; matrix products, arithmetic and copies ran while one was open for 5% of the time, Pallas kernels for 0%

commit v1 on v0

v1 whole, which is shorter than its diff:
```python
import functools

import jax
import jax.numpy as jnp
from jax import lax
from jax.experimental import pallas as pl
from jax.experimental.pallas import tpu as pltpu
from jax.sharding import PartitionSpec as P

EPSILON = 0.05
TEMP_TAU = 0.1
LOG2E = 1.4426950408889634
LN2 = 0.6931471805599453
MESH = pl.DeviceIdType.MESH
F32 = jnp.float32
BF16 = jnp.bfloat16


def groups(x):
    return x.reshape(x.shape[0] // 8, 8, x.shape[1])


def kernel(n_rows_total, z1_hbm, z2_hbm, c_hbm,
           q1_out, q2_out, loss_out, g1_out, g2_out, gp_out,
           z_ref, c_ref, e_ref, f_ref, x_ref, h_ref, d_ref, r_ref, s_ref, l_ref,
           csum_ref, csend_ref, crecv_ref, gsend_ref, grecv_ref, lbuf_ref,
           zsem, csem, ag_send, ag_recv, ex_send, ex_recv, gp_send, gp_recv, ls_send, ls_recv):
    rows = z1_hbm.shape[0]
    cols = c_hbm.shape[0]
    allc = 4 * cols
    p = lax.axis_index("proto")
    d = lax.axis_index("data")
    px = p + 1 - 2 * lax.rem(p, 2)
    py = lax.rem(p + 2, 4)
    pd = 3 - p
    sib = 1 - d
    grad_scale = 1.0 / (2.0 * n_rows_total * TEMP_TAU)

    barrier = pltpu.get_barrier_semaphore()
    peers = [(p, sib)] + [(q, e) for q in (px, py, pd) for e in (d, sib)]
    for q, e in peers:
        pl.semaphore_signal(barrier, inc=1, device_id=(q, e), device_id_type=MESH)
    cc = pltpu.make_async_copy(c_hbm, c_ref.at[pl.ds(0, cols)], csem)
    cc.start()
    zc = [pltpu.make_async_copy(z, z_ref.at[v], zsem.at[v]) for v, z in enumerate((z1_hbm, z2_hbm))]
    for k in zc:
        k.start()
    cc.wait()
    pl.semaphore_wait(barrier, 7)
    ag = []
    for i, q in enumerate((px, py, pd)):
        k = pltpu.make_async_remote_copy(
            src_ref=c_ref.at[pl.ds(0, cols)], dst_ref=c_ref.at[pl.ds((i + 1) * cols, cols)],
            send_sem=ag_send.at[i], recv_sem=ag_recv.at[i], device_id=(q, d), device_id_type=MESH)
        k.start()
        ag.append(k)
    for k in zc:
        k.wait()

    def exchange(v, i):
        return pltpu.make_async_remote_copy(
            src_ref=csend_ref.at[i, v], dst_ref=crecv_ref.at[i, v],
            send_sem=ex_send.at[i, v], recv_sem=ex_recv.at[i, v],
            device_id=(p, sib), device_id_type=MESH)

    def send_sum(v, i, total):
        csend_ref[i, v] = jnp.broadcast_to(jnp.sum(total, axis=0, keepdims=True), total.shape)
        exchange(v, i).start()

    def recv_weight(v, i):
        exchange(v, i).wait()
        return 1.0 / (csend_ref[i, v] + crecv_ref[i, v])

    TA = 512
    for j in range(4):
        if j:
            ag[j - 1].wait_recv()
        lanes = pl.ds(j * cols, cols)
        for v in range(2):
            def score_tile(t, acc, v=v, j=j, lanes=lanes):
                rs = pl.ds(pl.multiple_of(t * TA, TA), TA)
                s = lax.dot_general(z_ref[v, rs, :], c_ref[lanes, :], (((1,), (1,)), ((), ())),
                                    preferred_element_type=F32)
                x = s * (LOG2E / TEMP_TAU)
                f = jnp.exp2(x)
                e = f * f
                f_ref[v, rs, lanes] = f
                e_ref[v, rs, lanes] = e
                if j == 0:
                    x_ref[v, rs, :] = x
                half = f[:, :128] + f[:, 128:]
                if j == 0:
                    d_ref[v, rs, :] = half
                else:
                    d_ref[v, rs, :] += half
                return acc + jnp.sum(groups(e), axis=0)
            acc = lax.fori_loop(0, rows // TA, score_tile, jnp.zeros((8, cols), F32))
            csum_ref[v, :, lanes] = acc
            if j == 3:
                send_sum(v, 0, csum_ref[v])

    TB = 128

    def row_sums(v, t, w, store):
        rs = pl.ds(pl.multiple_of(t * TB, TB), TB)
        ew = groups(e_ref[v, rs, :]) * w[None]
        if store:
            e_ref[v, rs, :] = ew.reshape(TB, allc)
        r = jnp.sum(ew, axis=2, keepdims=True)
        return jnp.broadcast_to(r, (TB // 8, 8, 128))

    def col_sums(v, t, r, acc):
        rs = pl.ds(pl.multiple_of(t * TB, TB), TB)
        q = 1.0 / r
        e = e_ref[v, rs, :].reshape(TB // 8, 8, allc // 128, 128)
        eq = [jnp.sum(e[:, :, k, :] * q, axis=0) for k in range(allc // 128)]
        return acc + jnp.concatenate(eq, axis=1)

    nb = rows // TB
    for i in range(2):
        for v in range(2):
            w = recv_weight(v, i)

            def body(t, carry, v=v, w=w):
                r, acc = carry
                r_new = row_sums(v, t, w, False)
                acc = col_sums(v, t - 1, r, acc)
                return r_new, acc
            carry = (row_sums(v, 0, w, False), jnp.zeros((8, allc), F32))
            r, acc = lax.fori_loop(1, nb, body, carry)
            acc = col_sums(v, nb - 1, r, acc)
            send_sum(v, i + 1, acc)

    for v in range(2):
        w = recv_weight(v, 2)

        def last(t, _, v=v, w=w):
            rs = pl.ds(pl.multiple_of(t * TB, TB), TB)
            r = row_sums(v, t, w, True).reshape(TB, 128)
            dn = jnp.broadcast_to(jnp.sum(d_ref[v, rs, :], axis=1, keepdims=True), (TB, 128))
            r_ref[v, rs, :] = r
            d_ref[v, rs, :] = dn
            return 0
        lax.fori_loop(0, nb, last, 0)

    TC = 128

    def lanes2(a):
        return jnp.concatenate([a, a], axis=1)

    def own(t, acc):
        rs = pl.ds(pl.multiple_of(t * TC, TC), TC)
        qv, pv, lv = [], [], []
        for v in range(2):
            qv.append(1.0 / r_ref[v, rs, :])
            dn = d_ref[v, rs, :]
            pv.append(grad_scale / dn)
            lv.append(jnp.log(dn) * LOG2E)
            s_ref[v, rs, :] = qv[v] * grad_scale
            d_ref[v, rs, :] = pv[v]
        for v, out in ((0, q1_out), (1, q2_out)):
            o = 1 - v
            code = e_ref[v, rs, pl.ds(0, cols)] * lanes2(qv[v])
            out[rs, :] = code
            acc = acc + jnp.sum(groups((x_ref[o, rs, :] - lanes2(lv[o])) * code), axis=0)
            h_ref[o, rs, pl.ds(0, cols)] = (
                f_ref[o, rs, pl.ds(0, cols)] * lanes2(pv[o]) - code * grad_scale).astype(BF16)
        return acc
    lacc = lax.fori_loop(0, rows // TC, own, jnp.zeros((8, cols), F32))
    me = p * 2 + d
    lbuf_ref[me] = lacc[:, :128] + lacc[:, 128:]
    lcs = []
    for i, (q, e) in enumerate(peers):
        k = pltpu.make_async_remote_copy(
            src_ref=lbuf_ref.at[me], dst_ref=lbuf_ref.at[me],
            send_sem=ls_send.at[i], recv_sem=ls_recv.at[i],
            device_id=(q, e), device_id_type=MESH)
        k.start()
        lcs.append(k)
    tdims = (((0,), (0,)), ((), ()))
    gsend_ref[...] = (
        lax.dot_general(h_ref[0, :, pl.ds(0, cols)], z_ref[0], tdims, preferred_element_type=F32)
        + lax.dot_general(h_ref[1, :, pl.ds(0, cols)], z_ref[1], tdims, preferred_element_type=F32))
    gcopy = pltpu.make_async_remote_copy(
        src_ref=gsend_ref, dst_ref=grecv_ref, send_sem=gp_send, recv_sem=gp_recv,
        device_id=(p, sib), device_id_type=MESH)
    gcopy.start()

    TD = 256

    def rest(t, _):
        rs = pl.ds(pl.multiple_of(t * TD, TD), TD)
        for v, out in ((0, g1_out), (1, g2_out)):
            o = 1 - v
            pv = d_ref[v, rs, :]
            sv = s_ref[o, rs, :]
            hs = [h_ref[v, rs, pl.ds(0, cols)]]
            for j in range(1, 4):
                lanes = pl.ds(j * cols, cols)
                hs.append((f_ref[v, rs, lanes] * lanes2(pv) - e_ref[o, rs, lanes] * lanes2(sv)).astype(BF16))
            h = jnp.concatenate(hs, axis=1)
            out[rs, :] = jnp.dot(h, c_ref[...], preferred_element_type=F32)
        return 0
    lax.fori_loop(0, rows // TD, rest, 0)

    for k in lcs:
        k.wait()
    total = lbuf_ref[0]
    for i in range(1, 8):
        total = total + lbuf_ref[i]
    loss_out[0, 0] = jnp.sum(total) * (-LN2 / (2.0 * n_rows_total))
    gcopy.wait()
    gp_out[...] = gsend_ref[...] + grecv_ref[...]
    for k in ag:
        k.wait_send()


def solution(mesh):
    data_size = mesh.shape['data']

    def local_step(emb_one, emb_two, protos):
        rows, dim = emb_one.shape
        cols = protos.shape[0]
        allc = 4 * cols
        V = pltpu.VMEM
        out_shape = (
            V((rows, cols), F32), V((rows, cols), F32),
            jax.ShapeDtypeStruct((1, 1), F32),
            V((rows, dim), F32), V((rows, dim), F32),
            V((cols, dim), F32))
        vspec = pl.BlockSpec(memory_space=pltpu.VMEM)
        DMA = pltpu.SemaphoreType.DMA
        q1, q2, loss, g1, g2, gp = pl.pallas_call(
            functools.partial(kernel, rows * data_size),
            out_shape=out_shape,
            in_specs=[pl.BlockSpec(memory_space=pl.ANY)] * 3,
            out_specs=(vspec, vspec, pl.BlockSpec(memory_space=pltpu.SMEM), vspec, vspec, vspec),
            scratch_shapes=[
                V((2, rows, dim), BF16),
                V((allc, dim), BF16),
                V((2, rows, allc), F32),
                V((2, rows, allc), F32),
                V((2, rows, cols), F32),
                V((2, rows, cols), BF16),
                V((2, rows, 128), F32),
                V((2, rows, 128), F32),
                V((2, rows, 128), F32),
                V((8, 128), F32),
                V((2, 8, allc), F32),
                V((3, 2, 8, allc), F32),
                V((3, 2, 8, allc), F32),
                V((cols, dim), F32),
                V((cols, dim), F32),
                V((8, 8, 128), F32),
                DMA((2,)), DMA(()), DMA((3,)), DMA((3,)), DMA((3, 2)), DMA((3, 2)),
                DMA(()), DMA(()), DMA((7,)), DMA((7,)),
            ],
            compiler_params=pltpu.CompilerParams(collective_id=0, has_side_effects=True,
                                                 vmem_limit_bytes=52 * 1024 * 1024),
        )(emb_one, emb_two, protos)
        return q1, q2, loss.reshape(()), g1, g2, gp

    return jax.shard_map(
        local_step, mesh=mesh,
        in_specs=(P('data', None), P('data', None), P('proto', None)),
        out_specs=(P('data', 'proto'), P('data', 'proto'), P(), P('data', None), P('data', None), P('proto', None)),
        check_vma=False)
```

time: 240 us -> 63.1 us (0.26)
  blocking collectives: 102 us -> 0 us
  waiting for transfers between devices: 72.8 us -> 0 us
  Pallas kernels: 0 us -> 54.7 us
  other arithmetic: 25.6 us -> 0 us
  between operations: 17.3 us -> 2.33 us
  matrix products: 10.5 us -> 0 us
  local copies, waits for them, and re-layouts: 11.3 us -> 5.98 us
    psum x12 -> x0, blocking collectives: 102 us -> none  [the longest x6 66.5 us: view_terms(): row_sum = lax.psum(jnp.sum(transport, axis=1, keepdims=True), 'proto')]
    psum x2 -> x0, waiting for transfers between devices: 72.8 us -> none  [the longest x1 72.8 us: local_step(): lax.psum(jnp.einsum('nk,kd->nd', logit_grad_one, protos, preferred_elemen...]
    pallas_call x0 -> x1, Pallas kernels: none -> 54.7 us  [local_step(): pl.pallas_call(functools.partial(kernel, rows * data_size), out_shape=out...]
    reduce_sum x11 -> x0, other arithmetic: 16.7 us -> none  [the longest x4 6 us: view_terms(): row_sum = lax.psum(jnp.sum(transport, axis=1, keepdims=True), 'proto')]
    dot_general x6 -> x0, matrix products: 10.5 us -> none  [the longest x2 3.93 us: view_terms(): jnp.einsum('nd,kd->nk', emb, protos, preferred_element_type=jnp.float32)]
    convert_element_type x2 -> x0, other arithmetic: 8.85 us -> none  [the longest x1 4.56 us: local_step(): ((jnp.exp(logp_one) - codes_two) / grad_scale).astype(jnp.bfloat16)]
    unnamed x27 -> x5, local copies, waits for them, and re-layouts: 11.3 us -> 5.98 us
  transfers between devices with their start and end apart: 2 -> 0, of which waited for: 1 -> 0; matrix products, arithmetic and copies ran while one was open for 5% -> 0% of each run, Pallas kernels for 0% -> 0%
where the time goes in v1:
time: 63.1 us; the launch traced here: 63 us
  Pallas kernels  54.7 us (87%)
  local copies, waits for them, and re-layouts  5.98 us (9%)
  between operations  2.33 us (4%)
    pallas_call x1, Pallas kernels, local_step(): pl.pallas_call(functools.partial(kernel, rows * data_size), out_shape=out...  54.7 us
    unnamed x5, local copies, waits for them, and re-layouts  5.98 us

profile of v1, /device:TPU:0, one launch (start us, length us, event | category | flops | bytes accessed | tf_op | source)
XLA Modules:
  0.0 63.0 jit_solution(5680090891828583769)
XLA Ops:
  0.6 54.7 %shard_map.82 = (f32[2048,256]{1,0:T(8,128)S(1)}, f32[2048,256]{1,0:T(8,128)S(1)}, f32[1,1]{1,0:T(1,128)}, f32[2048,256]{1,0:T(8,128)S(1)}, f32[2048,256]{1,0:T(8,128)S(1)}, /*index=5*/f32[256,256]{1,0:T(8,128)S(1)}) custom-call(bf16[2048,256]{1,0:T(8,128)(2,1)} %z1_hbm.1, bf16[2048,256]{1,0:T(8,128)(2,1)} %z2_hbm.1, bf16[256,256]{1,0:T(8,128)(2,1)} %c_hbm.1), custom_call_target="tpu_custom_call" | custom-call | tf_op jit(solution)/shard_map/pallas_call | solution.py:233
  55.3 1.3 %copy.15 = f32[2048,256]{1,0:T(8,128)} copy(f32[2048,256]{1,0:T(8,128)S(1)} %get-tuple-element.18) | data formatting | bytes 4194304
  56.6 0.7 %copy.19 = f32[256,256]{1,0:T(8,128)} copy(f32[256,256]{1,0:T(8,128)S(1)} %get-tuple-element.23) | data formatting | bytes 524288
  57.3 1.3 %copy.16 = f32[2048,256]{1,0:T(8,128)} copy(f32[2048,256]{1,0:T(8,128)S(1)} %get-tuple-element.19) | data formatting | bytes 4194304
  58.7 1.3 %copy.17 = f32[2048,256]{1,0:T(8,128)} copy(f32[2048,256]{1,0:T(8,128)S(1)} %get-tuple-element.21) | data formatting | bytes 4194304
  60.0 1.3 %copy.18 = f32[2048,256]{1,0:T(8,128)} copy(f32[2048,256]{1,0:T(8,128)S(1)} %get-tuple-element.22) | data formatting | bytes 4194304

commit v2 on v1

--- a/solution.py
+++ b/solution.py
@@ -22,7 +22,7 @@
 
 def kernel(n_rows_total, z1_hbm, z2_hbm, c_hbm,
            q1_out, q2_out, loss_out, g1_out, g2_out, gp_out,
-           z_ref, c_ref, e_ref, f_ref, x_ref, h_ref, d_ref, r_ref, s_ref, l_ref,
+           z_ref, c_ref, e_ref, f_ref, x_ref, h_ref, d_ref, r_ref,
            csum_ref, csend_ref, crecv_ref, gsend_ref, grecv_ref, lbuf_ref,
            zsem, csem, ag_send, ag_recv, ex_send, ex_recv, gp_send, gp_recv, ls_send, ls_recv):
     rows = z1_hbm.shape[0]
@@ -71,7 +71,7 @@
         exchange(v, i).wait()
         return 1.0 / (csend_ref[i, v] + crecv_ref[i, v])
 
-    TA = 512
+    TA = 2048
     for j in range(4):
         if j:
             ag[j - 1].wait_recv()
@@ -88,58 +88,61 @@
                 e_ref[v, rs, lanes] = e
                 if j == 0:
                     x_ref[v, rs, :] = x
-                half = f[:, :128] + f[:, 128:]
-                if j == 0:
-                    d_ref[v, rs, :] = half
-                else:
-                    d_ref[v, rs, :] += half
                 return acc + jnp.sum(groups(e), axis=0)
             acc = lax.fori_loop(0, rows // TA, score_tile, jnp.zeros((8, cols), F32))
             csum_ref[v, :, lanes] = acc
             if j == 3:
                 send_sum(v, 0, csum_ref[v])
 
-    TB = 128
-
-    def row_sums(v, t, w, store):
-        rs = pl.ds(pl.multiple_of(t * TB, TB), TB)
-        ew = groups(e_ref[v, rs, :]) * w[None]
-        if store:
-            e_ref[v, rs, :] = ew.reshape(TB, allc)
-        r = jnp.sum(ew, axis=2, keepdims=True)
-        return jnp.broadcast_to(r, (TB // 8, 8, 128))
-
-    def col_sums(v, t, r, acc):
-        rs = pl.ds(pl.multiple_of(t * TB, TB), TB)
-        q = 1.0 / r
-        e = e_ref[v, rs, :].reshape(TB // 8, 8, allc // 128, 128)
-        eq = [jnp.sum(e[:, :, k, :] * q, axis=0) for k in range(allc // 128)]
-        return acc + jnp.concatenate(eq, axis=1)
-
+    TB = 256
     nb = rows // TB
+    nk = allc // 128
+
+    def tile(t, n):
+        return pl.ds(pl.multiple_of(t * n, n), n)
+
+    def row_sums(v, t, w):
+        rs = tile(t, TB)
+        part = groups(e_ref[v, rs, pl.ds(0, 128)]) * w[0][None]
+        for k in range(1, nk):
+            part = part + groups(e_ref[v, rs, pl.ds(k * 128, 128)]) * w[k][None]
+        r = jnp.broadcast_to(jnp.sum(part, axis=2, keepdims=True), part.shape)
+        r_ref[v, rs, :] = r.reshape(TB, 128)
+
+    def col_sums(v, t, acc):
+        rs = tile(t, TB)
+        q = 1.0 / groups(r_ref[v, rs, :])
+        return tuple(acc[k] + jnp.sum(groups(e_ref[v, rs, pl.ds(k * 128, 128)]) * q, axis=0)
+                     for k in range(nk))
+
+    def split(w):
+        return tuple(w[:, k * 128:(k + 1) * 128] for k in range(nk))
+
     for i in range(2):
         for v in range(2):
-            w = recv_weight(v, i)
-
-            def body(t, carry, v=v, w=w):
-                r, acc = carry
-                r_new = row_sums(v, t, w, False)
-                acc = col_sums(v, t - 1, r, acc)
-                return r_new, acc
-            carry = (row_sums(v, 0, w, False), jnp.zeros((8, allc), F32))
-            r, acc = lax.fori_loop(1, nb, body, carry)
-            acc = col_sums(v, nb - 1, r, acc)
-            send_sum(v, i + 1, acc)
+            w = split(recv_weight(v, i))
+
+            def body(t, acc, v=v, w=w):
+                acc = col_sums(v, t - 1, acc)
+                row_sums(v, t, w)
+                return acc
+            row_sums(v, 0, w)
+            acc = lax.fori_loop(1, nb, body, (jnp.zeros((8, 128), F32),) * nk)
+            acc = col_sums(v, nb - 1, acc)
+            send_sum(v, i + 1, jnp.concatenate(acc, axis=1))
 
     for v in range(2):
-        w = recv_weight(v, 2)
+        wfull = recv_weight(v, 2)
+        csum_ref[v] = wfull
+        w = split(wfull)
 
         def last(t, _, v=v, w=w):
-            rs = pl.ds(pl.multiple_of(t * TB, TB), TB)
-            r = row_sums(v, t, w, True).reshape(TB, 128)
-            dn = jnp.broadcast_to(jnp.sum(d_ref[v, rs, :], axis=1, keepdims=True), (TB, 128))
-            r_ref[v, rs, :] = r
-            d_ref[v, rs, :] = dn
+            rs = tile(t, TB)
+            dsum = f_ref[v, rs, pl.ds(0, 128)]
+            for k in range(1, nk):
+                dsum = dsum + f_ref[v, rs, pl.ds(k * 128, 128)]
+            row_sums(v, t, w)
+            d_ref[v, rs, :] = jnp.broadcast_to(jnp.sum(dsum, axis=1, keepdims=True), (TB, 128))
             return 0
         lax.fori_loop(0, nb, last, 0)
 
@@ -148,19 +151,23 @@
     def lanes2(a):
         return jnp.concatenate([a, a], axis=1)
 
+    def scaled(v, rs, lanes):
+        n = rs.size
+        return (groups(e_ref[v, rs, lanes]) * csum_ref[v, :, lanes][None]).reshape(n, lanes.size)
+
     def own(t, acc):
-        rs = pl.ds(pl.multiple_of(t * TC, TC), TC)
+        rs = tile(t, TC)
         qv, pv, lv = [], [], []
         for v in range(2):
             qv.append(1.0 / r_ref[v, rs, :])
             dn = d_ref[v, rs, :]
             pv.append(grad_scale / dn)
-            lv.append(jnp.log(dn) * LOG2E)
-            s_ref[v, rs, :] = qv[v] * grad_scale
+            lv.append(jnp.log2(dn))
+            r_ref[v, rs, :] = qv[v] * grad_scale
             d_ref[v, rs, :] = pv[v]
         for v, out in ((0, q1_out), (1, q2_out)):
             o = 1 - v
-            code = e_ref[v, rs, pl.ds(0, cols)] * lanes2(qv[v])
+            code = scaled(v, rs, pl.ds(0, cols)) * lanes2(qv[v])
             out[rs, :] = code
             acc = acc + jnp.sum(groups((x_ref[o, rs, :] - lanes2(lv[o])) * code), axis=0)
             h_ref[o, rs, pl.ds(0, cols)] = (
@@ -189,17 +196,20 @@
     TD = 256
 
     def rest(t, _):
-        rs = pl.ds(pl.multiple_of(t * TD, TD), TD)
-        for v, out in ((0, g1_out), (1, g2_out)):
+        rs = tile(t, TD)
+        both = []
+        for v in range(2):
             o = 1 - v
             pv = d_ref[v, rs, :]
-            sv = s_ref[o, rs, :]
+            sv = r_ref[o, rs, :]
             hs = [h_ref[v, rs, pl.ds(0, cols)]]
             for j in range(1, 4):
                 lanes = pl.ds(j * cols, cols)
-                hs.append((f_ref[v, rs, lanes] * lanes2(pv) - e_ref[o, rs, lanes] * lanes2(sv)).astype(BF16))
-            h = jnp.concatenate(hs, axis=1)
-            out[rs, :] = jnp.dot(h, c_ref[...], preferred_element_type=F32)
+                hs.append((f_ref[v, rs, lanes] * lanes2(pv) - scaled(o, rs, lanes) * lanes2(sv)).astype(BF16))
+            both.append(jnp.concatenate(hs, axis=1))
+        g = jnp.dot(jnp.concatenate(both, axis=0), c_ref[...], preferred_element_type=F32)
+        g1_out[rs, :] = g[:TD]
+        g2_out[rs, :] = g[TD:]
         return 0
     lax.fori_loop(0, rows // TD, rest, 0)
 
@@ -244,8 +254,6 @@
                 V((2, rows, cols), BF16),
                 V((2, rows, 128), F32),
                 V((2, rows, 128), F32),
-                V((2, rows, 128), F32),
-                V((8, 128), F32),
                 V((2, 8, allc), F32),
                 V((3, 2, 8, allc), F32),
                 V((3, 2, 8, allc), F32),

time: 63.1 us -> 38.4 us (0.61)
  Pallas kernels: 54.7 us -> 30 us
    pallas_call x1, Pallas kernels: 54.7 us -> 30 us  [local_step(): pl.pallas_call(functools.partial(kernel, rows * data_size), out_shape=out...]
where the time goes in v2:
time: 38.4 us; the launch traced here: 38.3 us
  Pallas kernels  30 us (78%)
  local copies, waits for them, and re-layouts  5.98 us (16%)
  between operations  2.33 us (6%)
    pallas_call x1, Pallas kernels, local_step(): pl.pallas_call(functools.partial(kernel, rows * data_size), out_shape=out...  30 us
    unnamed x5, local copies, waits for them, and re-layouts  5.98 us

profile of v2, /device:TPU:0, one launch (start us, length us, event | category | flops | bytes accessed | tf_op | source)
XLA Modules:
  0.0 38.3 jit_solution(3918606518917840232)
XLA Ops:
  0.6 30.0 %shard_map.82 = (f32[2048,256]{1,0:T(8,128)S(1)}, f32[2048,256]{1,0:T(8,128)S(1)}, f32[1,1]{1,0:T(1,128)}, f32[2048,256]{1,0:T(8,128)S(1)}, f32[2048,256]{1,0:T(8,128)S(1)}, /*index=5*/f32[256,256]{1,0:T(8,128)S(1)}) custom-call(bf16[2048,256]{1,0:T(8,128)(2,1)} %z1_hbm.1, bf16[2048,256]{1,0:T(8,128)(2,1)} %z2_hbm.1, bf16[256,256]{1,0:T(8,128)(2,1)} %c_hbm.1), custom_call_target="tpu_custom_call" | custom-call | tf_op jit(solution)/shard_map/pallas_call | solution.py:243
  30.6 1.3 %copy.15 = f32[2048,256]{1,0:T(8,128)} copy(f32[2048,256]{1,0:T(8,128)S(1)} %get-tuple-element.18) | data formatting | bytes 4194304
  31.9 0.7 %copy.19 = f32[256,256]{1,0:T(8,128)} copy(f32[256,256]{1,0:T(8,128)S(1)} %get-tuple-element.23) | data formatting | bytes 524288
  32.6 1.3 %copy.16 = f32[2048,256]{1,0:T(8,128)} copy(f32[2048,256]{1,0:T(8,128)S(1)} %get-tuple-element.19) | data formatting | bytes 4194304
  33.9 1.3 %copy.17 = f32[2048,256]{1,0:T(8,128)} copy(f32[2048,256]{1,0:T(8,128)S(1)} %get-tuple-element.21) | data formatting | bytes 4194304
  35.3 1.3 %copy.18 = f32[2048,256]{1,0:T(8,128)} copy(f32[2048,256]{1,0:T(8,128)S(1)} %get-tuple-element.22) | data formatting | bytes 4194304
